TPU v7x, 32 devices: a whole 2x2x4 slice. The times are simulated.
32 devices in a mesh: row: 8 (over z, core), col: 4 (over y, x).
Axes of the slice: x: 2, y: 2, z: 4, core: 2. Of those that a mesh axis runs over, the one named last changes fastest.
Arguments:
- vectors: bfloat16 [2, 4, 16384], P(None, 'col', 'row'), may hold values from -6 to 6
- lr_left: bfloat16 [8, 4, 32, 8, 2048], P('row', 'col'), may hold values from -0.75 to 0.75
- lr_right: bfloat16 [8, 4, 32, 8, 2048], P('row', 'col'), may hold values from -0.125 to 0.125
- tile_rank: int32 [8, 4, 32], P('row', 'col'), may hold values from 0 to 8, as said below
- leaf_values: bfloat16 [8, 4, 8, 512, 512], P('row', 'col'), may hold values from -0.25 to 0.25
- leaf_places: int32 [8, 4, 8, 2], P('row', 'col'), may hold values from 0 to 31, as said below
- cluster_perm: int32 [8, 8192], P('row'), may hold values from 0 to 65535, as said below
- kappa: float32 [32, 16, 128], P('row', 'col'), may hold values from 0.25 to 4
Outputs:
- prior_action: float32 [2, 32, 16, 128], P(None, 'row', 'col')
Inputs may be any that keep to these rules, and one draw needn't show every extreme that they name: `tile_rank`: 0 exactly on the tiles that contain a leaf, 1 to 8 on the others. `leaf_places`: the 8 leaves of a block are distinct; entry 0 indexes rows and entry 1 column of the block in units of 512. `cluster_perm`: a permutation of all brick indices; within each aligned block of 2048 entries, every value of entry // 2048 occurs exactly 128 times or not at all.
All inputs are finite; a program needn't handle non-finite values.
Results may differ from a plain program's by a relative error of at most 0.0023.
Values may be sent and summed in bfloat16 or wider, within the bound.
A program may use at most 64 MiB of HBM per device.

v0:
```python
import jax
import jax.numpy as jnp
from jax import lax
from jax.sharding import PartitionSpec as P

NVEC = 2
CX = 4
CY = 4
NZ = 128
TILE_ROWS = 4
TILE_COLS = 8
KMAX = 8
LEAF = 512


def extended(cells, sides, width):
    for axis, dim in sides:
        count = lax.axis_size(axis)
        ends = count - 1
        head = lax.slice_in_dim(cells, 0, width, axis=dim)
        tail = lax.slice_in_dim(cells, cells.shape[dim] - width, cells.shape[dim], axis=dim)
        cells = jnp.concatenate(
            [
                lax.ppermute(tail, axis, [(i, (i + 1) % count) for i in range(ends)]),
                cells,
                lax.ppermute(head, axis, [((i + 1) % count, i) for i in range(ends)]),
            ],
            axis=dim,
        )
    return cells


def prior_step(padded, stiffness):
    center = padded[:, 1:-1, 1:-1, :]
    flat_pad = jnp.pad(center, ((0, 0), (0, 0), (0, 0), (1, 1)))
    beside = padded[:, 2:, 1:-1, :] + padded[:, :-2, 1:-1, :]
    beside = beside + padded[:, 1:-1, 2:, :] + padded[:, 1:-1, :-2, :]
    beside = beside + flat_pad[..., 2:] + flat_pad[..., :-2]
    return ((6.0 + stiffness) * center - beside) * 0.125


def route(values, targets, groups, points, capacity, devices):
    target_dev = targets // points
    places = targets % points
    grouped = target_dev.reshape(groups, points)
    one_hot = (grouped[:, :, None] == jnp.arange(devices)[None, None, :]).astype(jnp.int32)
    running = jnp.cumsum(one_hot, axis=1)
    within = jnp.sum(running * one_hot, axis=2) - 1
    slot_index = jnp.arange(groups)[:, None] * capacity + within
    buffer_at = (grouped * (groups * capacity) + slot_index).reshape(-1)
    buffer_len = devices * groups * capacity
    send_values = jnp.zeros((values.shape[0], buffer_len), jnp.float32).at[:, buffer_at].set(values)
    send_places = jnp.full((1, buffer_len), points, jnp.int32).at[0, buffer_at].set(places)
    return (send_values, send_places)


def per_device(
    vectors, lr_left, lr_right, tile_rank, leaf_values, leaf_places, cluster_perm, kappa
):
    gathered = lax.all_gather(vectors, "row", axis=2, tiled=True)
    x_column = gathered[:, 0, :]
    tile_size = lr_left.shape[-1]
    rows_len = tile_size * TILE_ROWS
    x_tiles = x_column.reshape(NVEC, TILE_COLS, tile_size)
    far_right = lr_right[0, 0].reshape(TILE_ROWS, TILE_COLS, KMAX, tile_size)
    projected = jnp.einsum("abkp,vbp->abvk", far_right, x_tiles, preferred_element_type=jnp.float32)
    rank_mask = (
        jnp.arange(KMAX)[None, None, :] < tile_rank[0, 0].reshape(TILE_ROWS, TILE_COLS)[:, :, None]
    ).astype(jnp.float32)
    projected = (projected * rank_mask[:, :, None, :]).astype(jnp.bfloat16)
    far_left = lr_left[0, 0].reshape(TILE_ROWS, TILE_COLS, KMAX, tile_size)
    far_part = jnp.einsum(
        "abkp,abvk->vap", far_left, projected, preferred_element_type=jnp.float32
    ).reshape(NVEC, rows_len)
    leaf_pos = leaf_places[0, 0]
    x_sub = x_column.reshape(NVEC, x_column.shape[1] // LEAF, LEAF)
    picked = jnp.take(x_sub, leaf_pos[:, 1], axis=1)
    near_out = jnp.einsum(
        "lqp,vlp->vlq", leaf_values[0, 0], picked, preferred_element_type=jnp.float32
    )
    selector = (leaf_pos[:, 0][:, None] == jnp.arange(rows_len // LEAF)[None, :]).astype(
        jnp.float32
    )
    near_part = jnp.einsum("vlq,lr->vrq", near_out, selector, precision=lax.Precision.HIGHEST)
    partial_sums = far_part + near_part.reshape(NVEC, rows_len)
    points = vectors.shape[2]
    devices = lax.axis_size("row") * lax.axis_size("col")
    capacity = 2 * points // devices
    summed = lax.psum_scatter(partial_sums, "col", scatter_dimension=1, tiled=True)
    targets = lax.dynamic_slice_in_dim(cluster_perm[0], lax.axis_index("col") * points, points)
    send_values, send_places = route(summed, targets, 1, points, capacity, devices)
    received_values, received_places = (
        lax.all_to_all(send_values, ("row", "col"), split_axis=1, concat_axis=1, tiled=True),
        lax.all_to_all(send_places, ("row", "col"), split_axis=1, concat_axis=1, tiled=True),
    )
    field = (
        jnp.zeros((NVEC, points + 1), jnp.float32).at[:, received_places[0]].add(received_values)
    )
    field = field[:, :points].reshape(NVEC, CX, CY, NZ)
    for repeat in range(4):
        padded = extended(field, (("row", 1), ("col", 2)), 1)
        field = prior_step(padded, kappa)
    return field


def solution(mesh):
    in_specs = (
        P(None, "col", "row"),
        P("row", "col", None, None, None),
        P("row", "col", None, None, None),
        P("row", "col", None),
        P("row", "col", None, None, None),
        P("row", "col", None, None),
        P("row", None),
        P("row", "col", None),
    )
    out_specs = P(None, "row", "col", None)
    return jax.shard_map(
        per_device, mesh=mesh, in_specs=in_specs, out_specs=out_specs, check_vma=False
    )
```

profile of v0, /device:TPU:12, one launch (start us, length us, event | category | flops | bytes accessed | tf_op | source)
XLA Modules:
  0.0 208.1 jit_solution(8211785777179416884)
XLA Ops:
  8.0 14.4 %all_gather.3 = bf16[2,1,16384]{2,0,1:T(2,128)(2,1)S(1)} all-gather(bf16[2,1,2048]{2,0,1:T(2,128)(2,1)} %param.8), channel_id=1, replica_groups=mesh['row'=8,'col'=4] {'row'}, dimensions={2}, use_global_device_ids=true | all-gather | bytes 73728 | tf_op jit(solution)/shard_map/all_gather | solution.py:60
  23.1 3.5 %fusion.2 = f32[2,8,512]{2,0,1:T(2,128)S(1)} fusion(bf16[1,1,8,512,512]{4,3,2,1,0:T(8,128)(2,1)} %param.12, bf16[8,2,512]{2,1,0:T(2,128)(2,1)S(1)} %gather_fusion, pred[8]{0:T(512)(128)(4,1)S(1)} %and_bitcast_fusion), kind=kOutput, calls=%fused_computation.7 | convolution fusion | flops 8396800 | bytes 4243464 | tf_op jit(solution)/shard_map/lqp,vlp->vlq/dot_general | solution.py:78
  28.2 2.8 %fusion.7 = f32[4,2,2048,1]{2,1,3,0:T(2,128)S(1)} fusion(bf16[4,8,8,2048]{3,2,1,0:T(8,128)(2,1)S(1)} %bitcast.79, bf16[2,8,2048,1]{2,0,1,3:T(2,128)(2,1)S(1)} %bitcast.87, bf16[4,8,8,2048]{3,2,1,0:T(8,128)(2,1)S(1)} %bitcast.84, f32[4,8,8]{2,1,0:T(8,128)S(1)} %fusion.42), kind=kOutput, calls=%fused_computation.11 | convolution fusion | flops 4195328 | bytes 2229248 | tf_op jit(solution)/shard_map/abkp,abvk->vap/dot_general | solution.py:72
  31.0 2.7 %copy.53 = f32[2,8192]{0,1:T(8,128)} copy(f32[2,8192]{1,0:T(2,128)S(1)} %add.151) | data formatting | bytes 131072
  34.5 9.1 %reduce-window.6 = s32[1,32,16,128]{3,2,1,0:T(8,128)S(1)} reduce-window(s32[1,32,16,128]{3,2,1,0:T(8,128)S(1)} %bitcast.83, s32[]{:T(128)} %constant.61.clone.1), window={size=1x1x1x128 pad=0_0x0_0x0_0x127_0}, to_apply=%region_0.1 | reduce-window | flops 8323072 | bytes 524292 | tf_op jit(solution)/shard_map/reduce-window
  44.8 8.6 %scatter_custom_fusion.2 = s32[4096]{0:T(1024)} fusion(s32[2048]{0:T(1024)S(1)} %broadcast_select_fusion.2, s32[2048]{0:T(1024)S(1)} %get-tuple-element.29, s32[]{:T(128)} %constant.60.clone.1), kind=kCustom, calls=%fused_computation.107 | custom fusion | bytes 16388
  53.4 5.8 %all-to-all-start = ((s32[1,32,128]{2,0,1:T(1,128)}), s32[1,32,128]{2,0,1:T(1,128)S(1)}, u32[]{:S(2)}, u32[]{:S(2)}) async-start(s32[1,32,128]{2,0,1:T(1,128)} %bitcast.7), calls=%async_computation | async-start | bytes 32768 | tf_op jit(solution)/shard_map/all_to_all | solution.py:94
  59.2 28.3 %reduce-scatter.4.cloned.1.call-done = f32[2048,2]{1,0:T(8,128)} async-done(((f32[8192,2]{1,0:T(8,128)}), f32[2048,2]{1,0:T(8,128)}) %reduce-scatter.4.cloned.1.call-update) | async-done | bytes 16400
  90.5 6.5 %scatter_custom_fusion = f32[2,4096]{0,1:T(8,128)S(1)} fusion(s32[2048]{0:T(1024)S(1)} %bitcast.91, f32[2048,2]{1,0:T(8,128)} %copy.42, f32[]{:T(128)} %constant.59.clone.1), kind=kCustom, calls=%fused_computation.12 | custom fusion | bytes 33280 | tf_op jit(solution)/shard_map/scatter | solution.py:52
  98.1 4.9 %all-to-all-start.1 = ((f32[2,32,128]{2,0,1:T(2,128)}), f32[2,32,128]{2,0,1:T(2,128)S(1)}, u32[]{:S(2)}, u32[]{:S(2)}) async-start(f32[2,32,128]{2,0,1:T(2,128)} %copy.43), calls=%async_computation.1 | async-start | bytes 65536 | tf_op jit(solution)/shard_map/all_to_all | solution.py:93
  103.1 5.1 %all-to-all-done.1 = f32[2,32,128]{2,0,1:T(2,128)S(1)} async-done(((f32[2,32,128]{2,0,1:T(2,128)}), f32[2,32,128]{2,0,1:T(2,128)S(1)}, u32[]{:S(2)}, u32[]{:S(2)}) %all-to-all-start.1) | async-done | bytes 32800 | tf_op jit(solution)/shard_map/all_to_all | solution.py:93
  108.2 2.0 copy.44
  110.2 26.0 %scatter_custom_fusion.1 = f32[2,2049]{0,1:T(8,128)S(1)} fusion(s32[4096]{0:T(1024)S(1)} %bitcast.96, f32[4096,2]{1,0:T(8,128)} %copy.44, f32[]{:T(128)} %constant.59.clone.1), kind=kCustom, calls=%fused_computation.14 | custom fusion | flops 8192 | bytes 16904 | tf_op jit(solution)/shard_map/scatter-add | solution.py:97
  136.6 3.0 %collective-permute-start = (f32[2,1,4,128]{3,2,1,0:T(4,128)S(1)}, f32[2,1,4,128]{3,2,1,0:T(4,128)S(1)}, u32[]{:S(2)}, u32[]{:S(2)}) collective-permute-start(f32[2,1,4,128]{3,2,1,0:T(4,128)S(1)} %get-tuple-element.26), channel_id=1, source_target_pairs={{4,0},{8,4},{12,8},{16,12},{20,16},{24,20},{28,24},{5,1},{9,5},{13... | collective-permute-start | bytes 12296 | tf_op jit(solution)/shard_map/ppermute | solution.py:26
  141.5 3.0 %collective-permute-done.1 = f32[2,1,4,128]{3,2,1,0:T(4,128)S(1)} collective-permute-done((f32[2,1,4,128]{3,2,1,0:T(4,128)S(1)}, f32[2,1,4,128]{3,2,1,0:T(4,128)S(1)}, u32[]{:S(2)}, u32[]{:S(2)}) %collective-permute-start.1) | collective-permute-done | bytes 4128 | tf_op jit(solution)/shard_map/ppermute | solution.py:24
  144.5 3.4 %collective-permute-start.2 = (f32[2,6,1,128]{3,2,1,0:T(1,128)S(1)}, f32[2,6,1,128]{3,2,1,0:T(1,128)S(1)}, u32[]{:S(2)}, u32[]{:S(2)}) collective-permute-start(f32[2,6,1,128]{3,2,1,0:T(1,128)S(1)} %get-tuple-element.17), channel_id=1, source_target_pairs={{1,0},{2,1},{3,2},{5,4},{6,5},{7,6},{9,8},{10,9},{11,10},{13,12},{... | collective-permute-start | bytes 18440 | tf_op jit(solution)/shard_map/ppermute | solution.py:26
  147.9 2.5 %collective-permute-start.3 = (f32[2,6,1,128]{3,2,1,0:T(1,128)S(1)}, f32[2,6,1,128]{3,2,1,0:T(1,128)S(1)}, u32[]{:S(2)}, u32[]{:S(2)}) collective-permute-start(f32[2,6,1,128]{3,2,1,0:T(1,128)S(1)} %get-tuple-element.18), channel_id=1, source_target_pairs={{0,1},{1,2},{2,3},{4,5},{5,6},{6,7},{8,9},{9,10},{10,11},{12,13},{... | collective-permute-start | bytes 18440 | tf_op jit(solution)/shard_map/ppermute | solution.py:24
  150.4 3.9 %collective-permute-done.3 = f32[2,6,1,128]{3,2,1,0:T(1,128)S(1)} collective-permute-done((f32[2,6,1,128]{3,2,1,0:T(1,128)S(1)}, f32[2,6,1,128]{3,2,1,0:T(1,128)S(1)}, u32[]{:S(2)}, u32[]{:S(2)}) %collective-permute-start.3) | collective-permute-done | bytes 6176 | tf_op jit(solution)/shard_map/ppermute | solution.py:24
  156.4 2.4 %collective-permute-start.5 = (f32[2,1,4,128]{3,2,1,0:T(4,128)S(1)}, f32[2,1,4,128]{3,2,1,0:T(4,128)S(1)}, u32[]{:S(2)}, u32[]{:S(2)}) collective-permute-start(f32[2,1,4,128]{3,2,1,0:T(4,128)S(1)} %get-tuple-element.23), channel_id=1, source_target_pairs={{0,4},{4,8},{8,12},{12,16},{16,20},{20,24},{24,28},{1,5},{5,9},{9,... | collective-permute-start | bytes 12296 | tf_op jit(solution)/shard_map/ppermute | solution.py:24
  158.8 2.5 %collective-permute-done.5 = f32[2,1,4,128]{3,2,1,0:T(4,128)S(1)} collective-permute-done((f32[2,1,4,128]{3,2,1,0:T(4,128)S(1)}, f32[2,1,4,128]{3,2,1,0:T(4,128)S(1)}, u32[]{:S(2)}, u32[]{:S(2)}) %collective-permute-start.5) | collective-permute-done | bytes 4128 | tf_op jit(solution)/shard_map/ppermute | solution.py:24
  161.3 2.2 %collective-permute-start.6 = (f32[2,6,1,128]{3,2,1,0:T(1,128)S(1)}, f32[2,6,1,128]{3,2,1,0:T(1,128)S(1)}, u32[]{:S(2)}, u32[]{:S(2)}) collective-permute-start(f32[2,6,1,128]{3,2,1,0:T(1,128)S(1)} %get-tuple-element.15), channel_id=1, source_target_pairs={{1,0},{2,1},{3,2},{5,4},{6,5},{7,6},{9,8},{10,9},{11,10},{13,12},{... | collective-permute-start | bytes 18440 | tf_op jit(solution)/shard_map/ppermute | solution.py:26
  163.5 3.6 %collective-permute-start.7 = (f32[2,6,1,128]{3,2,1,0:T(1,128)S(1)}, f32[2,6,1,128]{3,2,1,0:T(1,128)S(1)}, u32[]{:S(2)}, u32[]{:S(2)}) collective-permute-start(f32[2,6,1,128]{3,2,1,0:T(1,128)S(1)} %get-tuple-element.16), channel_id=1, source_target_pairs={{0,1},{1,2},{2,3},{4,5},{5,6},{6,7},{8,9},{9,10},{10,11},{12,13},{... | collective-permute-start | bytes 18440 | tf_op jit(solution)/shard_map/ppermute | solution.py:24
  167.2 2.8 %collective-permute-done.7 = f32[2,6,1,128]{3,2,1,0:T(1,128)S(1)} collective-permute-done((f32[2,6,1,128]{3,2,1,0:T(1,128)S(1)}, f32[2,6,1,128]{3,2,1,0:T(1,128)S(1)}, u32[]{:S(2)}, u32[]{:S(2)}) %collective-permute-start.7) | collective-permute-done | bytes 6176 | tf_op jit(solution)/shard_map/ppermute | solution.py:24
  170.1 1.9 collective-permute-start.8
  172.0 2.4 %collective-permute-start.9 = (f32[2,1,4,128]{3,2,1,0:T(4,128)S(1)}, f32[2,1,4,128]{3,2,1,0:T(4,128)S(1)}, u32[]{:S(2)}, u32[]{:S(2)}) collective-permute-start(f32[2,1,4,128]{3,2,1,0:T(4,128)S(1)} %get-tuple-element.21), channel_id=1, source_target_pairs={{0,4},{4,8},{8,12},{12,16},{16,20},{20,24},{24,28},{1,5},{5,9},{9,... | collective-permute-start | bytes 12296 | tf_op jit(solution)/shard_map/ppermute | solution.py:24
  174.4 2.5 %collective-permute-done.9 = f32[2,1,4,128]{3,2,1,0:T(4,128)S(1)} collective-permute-done((f32[2,1,4,128]{3,2,1,0:T(4,128)S(1)}, f32[2,1,4,128]{3,2,1,0:T(4,128)S(1)}, u32[]{:S(2)}, u32[]{:S(2)}) %collective-permute-start.9) | collective-permute-done | bytes 4128 | tf_op jit(solution)/shard_map/ppermute | solution.py:24
  178.9 3.9 %collective-permute-start.11 = (f32[2,6,1,128]{3,2,1,0:T(1,128)S(1)}, f32[2,6,1,128]{3,2,1,0:T(1,128)S(1)}, u32[]{:S(2)}, u32[]{:S(2)}) collective-permute-start(f32[2,6,1,128]{3,2,1,0:T(1,128)S(1)} %get-tuple-element.14), channel_id=1, source_target_pairs={{0,1},{1,2},{2,3},{4,5},{5,6},{6,7},{8,9},{9,10},{10,11},{12,13},{... | collective-permute-start | bytes 18440 | tf_op jit(solution)/shard_map/ppermute | solution.py:24
  182.8 2.5 %collective-permute-done.11 = f32[2,6,1,128]{3,2,1,0:T(1,128)S(1)} collective-permute-done((f32[2,6,1,128]{3,2,1,0:T(1,128)S(1)}, f32[2,6,1,128]{3,2,1,0:T(1,128)S(1)}, u32[]{:S(2)}, u32[]{:S(2)}) %collective-permute-start.11) | collective-permute-done | bytes 6176 | tf_op jit(solution)/shard_map/ppermute | solution.py:24
  187.3 2.4 %collective-permute-start.13 = (f32[2,1,4,128]{3,2,1,0:T(4,128)S(1)}, f32[2,1,4,128]{3,2,1,0:T(4,128)S(1)}, u32[]{:S(2)}, u32[]{:S(2)}) collective-permute-start(f32[2,1,4,128]{3,2,1,0:T(4,128)S(1)} %get-tuple-element.19), channel_id=1, source_target_pairs={{0,4},{4,8},{8,12},{12,16},{16,20},{20,24},{24,28},{1,5},{5,9},{9,... | collective-permute-start | bytes 12296 | tf_op jit(solution)/shard_map/ppermute | solution.py:24
  189.7 2.5 %collective-permute-done.13 = f32[2,1,4,128]{3,2,1,0:T(4,128)S(1)} collective-permute-done((f32[2,1,4,128]{3,2,1,0:T(4,128)S(1)}, f32[2,1,4,128]{3,2,1,0:T(4,128)S(1)}, u32[]{:S(2)}, u32[]{:S(2)}) %collective-permute-start.13) | collective-permute-done | bytes 4128 | tf_op jit(solution)/shard_map/ppermute | solution.py:24
  194.2 3.9 %collective-permute-start.15 = (f32[2,6,1,128]{3,2,1,0:T(1,128)S(1)}, f32[2,6,1,128]{3,2,1,0:T(1,128)S(1)}, u32[]{:S(2)}, u32[]{:S(2)}) collective-permute-start(f32[2,6,1,128]{3,2,1,0:T(1,128)S(1)} %get-tuple-element.12), channel_id=1, source_target_pairs={{0,1},{1,2},{2,3},{4,5},{5,6},{6,7},{8,9},{9,10},{10,11},{12,13},{... | collective-permute-start | bytes 18440 | tf_op jit(solution)/shard_map/ppermute | solution.py:24
  198.1 2.5 %collective-permute-done.15 = f32[2,6,1,128]{3,2,1,0:T(1,128)S(1)} collective-permute-done((f32[2,6,1,128]{3,2,1,0:T(1,128)S(1)}, f32[2,6,1,128]{3,2,1,0:T(1,128)S(1)}, u32[]{:S(2)}, u32[]{:S(2)}) %collective-permute-start.15) | collective-permute-done | bytes 6176 | tf_op jit(solution)/shard_map/ppermute | solution.py:24
  (78 shorter events, 21.0 us)
Async XLA Ops:
  6.5 21.7 %copy-start = (bf16[1,1,32,8,2048]{4,3,2,1,0:T(8,128)(2,1)S(1)}, bf16[1,1,32,8,2048]{4,3,2,1,0:T(8,128)(2,1)}, u32[]{:S(2)}) copy-start(bf16[1,1,32,8,2048]{4,3,2,1,0:T(8,128)(2,1)} %param.9) | copy-start | bytes 3145732
  6.5 81.0 %reduce-scatter.4.cloned.1.call-start = ((), (), s32[]{:S(2)}) async-start(), calls=%async_computation.3 | async-start | bytes 5242880
  23.0 4.4 %copy-start.6 = (s32[1,1,32]{2,1,0:T(1,128)S(1)}, s32[1,1,32]{2,1,0:T(1,128)}, u32[]{:S(2)}) copy-start(s32[1,1,32]{2,1,0:T(1,128)} %param.11) | copy-start | bytes 388
  23.0 5.2 %copy-start.1 = (bf16[1,1,32,8,2048]{4,3,2,1,0:T(8,128)(2,1)S(1)}, bf16[1,1,32,8,2048]{4,3,2,1,0:T(8,128)(2,1)}, u32[]{:S(2)}) copy-start(bf16[1,1,32,8,2048]{4,3,2,1,0:T(8,128)(2,1)} %param.10) | copy-start | bytes 3145732
  33.7 0.8 copy-start.3
  33.7 10.9 %copy-start.4 = (s32[2]{0:T(128)S(1)}, s32[2]{0:T(128)}, u32[]{:S(2)}) copy-start(s32[2]{0:T(128)} %constant.93) | copy-start | bytes 28
  33.7 11.0 %copy-start.5 = (s32[2]{0:T(128)S(1)}, s32[2]{0:T(128)}, u32[]{:S(2)}) copy-start(s32[2]{0:T(128)} %constant.96) | copy-start | bytes 28
  53.4 44.7 %all-to-all-start = ((s32[1,32,128]{2,0,1:T(1,128)}), s32[1,32,128]{2,0,1:T(1,128)S(1)}, u32[]{:S(2)}, u32[]{:S(2)}) async-start(s32[1,32,128]{2,0,1:T(1,128)} %bitcast.7), calls=%async_computation | async-start | bytes 32768 | tf_op jit(solution)/shard_map/all_to_all | solution.py:94
  98.1 10.0 %all-to-all-start.1 = ((f32[2,32,128]{2,0,1:T(2,128)}), f32[2,32,128]{2,0,1:T(2,128)S(1)}, u32[]{:S(2)}, u32[]{:S(2)}) async-start(f32[2,32,128]{2,0,1:T(2,128)} %copy.43), calls=%async_computation.1 | async-start | bytes 65536 | tf_op jit(solution)/shard_map/all_to_all | solution.py:93
  110.2 40.2 %copy-start.2 = (f32[4,4,128]{2,1,0:T(4,128)S(1)}, f32[4,4,128]{2,1,0:T(4,128)}, u32[]{:S(2)}) copy-start(f32[4,4,128]{2,1,0:T(4,128)} %param.15) | copy-start | bytes 24580
  136.6 4.9 %collective-permute-start = (f32[2,1,4,128]{3,2,1,0:T(4,128)S(1)}, f32[2,1,4,128]{3,2,1,0:T(4,128)S(1)}, u32[]{:S(2)}, u32[]{:S(2)}) collective-permute-start(f32[2,1,4,128]{3,2,1,0:T(4,128)S(1)} %get-tuple-element.26), channel_id=1, source_target_pairs={{4,0},{8,4},{12,8},{16,12},{20,16},{24,20},{28,24},{5,1},{9,5},{13... | collective-permute-start | bytes 12296 | tf_op jit(solution)/shard_map/ppermute | solution.py:26
  139.6 4.9 %collective-permute-start.1 = (f32[2,1,4,128]{3,2,1,0:T(4,128)S(1)}, f32[2,1,4,128]{3,2,1,0:T(4,128)S(1)}, u32[]{:S(2)}, u32[]{:S(2)}) collective-permute-start(f32[2,1,4,128]{3,2,1,0:T(4,128)S(1)} %get-tuple-element.25), channel_id=1, source_target_pairs={{0,4},{4,8},{8,12},{12,16},{16,20},{20,24},{24,28},{1,5},{5,9},{9,... | collective-permute-start | bytes 12296 | tf_op jit(solution)/shard_map/ppermute | solution.py:24
  144.5 5.9 %collective-permute-start.2 = (f32[2,6,1,128]{3,2,1,0:T(1,128)S(1)}, f32[2,6,1,128]{3,2,1,0:T(1,128)S(1)}, u32[]{:S(2)}, u32[]{:S(2)}) collective-permute-start(f32[2,6,1,128]{3,2,1,0:T(1,128)S(1)} %get-tuple-element.17), channel_id=1, source_target_pairs={{1,0},{2,1},{3,2},{5,4},{6,5},{7,6},{9,8},{10,9},{11,10},{13,12},{... | collective-permute-start | bytes 18440 | tf_op jit(solution)/shard_map/ppermute | solution.py:26
  147.9 6.4 %collective-permute-start.3 = (f32[2,6,1,128]{3,2,1,0:T(1,128)S(1)}, f32[2,6,1,128]{3,2,1,0:T(1,128)S(1)}, u32[]{:S(2)}, u32[]{:S(2)}) collective-permute-start(f32[2,6,1,128]{3,2,1,0:T(1,128)S(1)} %get-tuple-element.18), channel_id=1, source_target_pairs={{0,1},{1,2},{2,3},{4,5},{5,6},{6,7},{8,9},{9,10},{10,11},{12,13},{... | collective-permute-start | bytes 18440 | tf_op jit(solution)/shard_map/ppermute | solution.py:24
  154.5 4.3 %collective-permute-start.4 = (f32[2,1,4,128]{3,2,1,0:T(4,128)S(1)}, f32[2,1,4,128]{3,2,1,0:T(4,128)S(1)}, u32[]{:S(2)}, u32[]{:S(2)}) collective-permute-start(f32[2,1,4,128]{3,2,1,0:T(4,128)S(1)} %get-tuple-element.24), channel_id=1, source_target_pairs={{4,0},{8,4},{12,8},{16,12},{20,16},{24,20},{28,24},{5,1},{9,5},{13... | collective-permute-start | bytes 12296 | tf_op jit(solution)/shard_map/ppermute | solution.py:26
  156.4 4.9 %collective-permute-start.5 = (f32[2,1,4,128]{3,2,1,0:T(4,128)S(1)}, f32[2,1,4,128]{3,2,1,0:T(4,128)S(1)}, u32[]{:S(2)}, u32[]{:S(2)}) collective-permute-start(f32[2,1,4,128]{3,2,1,0:T(4,128)S(1)} %get-tuple-element.23), channel_id=1, source_target_pairs={{0,4},{4,8},{8,12},{12,16},{16,20},{20,24},{24,28},{1,5},{5,9},{9,... | collective-permute-start | bytes 12296 | tf_op jit(solution)/shard_map/ppermute | solution.py:24
  161.3 5.9 %collective-permute-start.6 = (f32[2,6,1,128]{3,2,1,0:T(1,128)S(1)}, f32[2,6,1,128]{3,2,1,0:T(1,128)S(1)}, u32[]{:S(2)}, u32[]{:S(2)}) collective-permute-start(f32[2,6,1,128]{3,2,1,0:T(1,128)S(1)} %get-tuple-element.15), channel_id=1, source_target_pairs={{1,0},{2,1},{3,2},{5,4},{6,5},{7,6},{9,8},{10,9},{11,10},{13,12},{... | collective-permute-start | bytes 18440 | tf_op jit(solution)/shard_map/ppermute | solution.py:26
  163.5 6.4 %collective-permute-start.7 = (f32[2,6,1,128]{3,2,1,0:T(1,128)S(1)}, f32[2,6,1,128]{3,2,1,0:T(1,128)S(1)}, u32[]{:S(2)}, u32[]{:S(2)}) collective-permute-start(f32[2,6,1,128]{3,2,1,0:T(1,128)S(1)} %get-tuple-element.16), channel_id=1, source_target_pairs={{0,1},{1,2},{2,3},{4,5},{5,6},{6,7},{8,9},{9,10},{10,11},{12,13},{... | collective-permute-start | bytes 18440 | tf_op jit(solution)/shard_map/ppermute | solution.py:24
  170.1 4.3 %collective-permute-start.8 = (f32[2,1,4,128]{3,2,1,0:T(4,128)S(1)}, f32[2,1,4,128]{3,2,1,0:T(4,128)S(1)}, u32[]{:S(2)}, u32[]{:S(2)}) collective-permute-start(f32[2,1,4,128]{3,2,1,0:T(4,128)S(1)} %get-tuple-element.22), channel_id=1, source_target_pairs={{4,0},{8,4},{12,8},{16,12},{20,16},{24,20},{28,24},{5,1},{9,5},{13... | collective-permute-start | bytes 12296 | tf_op jit(solution)/shard_map/ppermute | solution.py:26
  172.0 4.9 %collective-permute-start.9 = (f32[2,1,4,128]{3,2,1,0:T(4,128)S(1)}, f32[2,1,4,128]{3,2,1,0:T(4,128)S(1)}, u32[]{:S(2)}, u32[]{:S(2)}) collective-permute-start(f32[2,1,4,128]{3,2,1,0:T(4,128)S(1)} %get-tuple-element.21), channel_id=1, source_target_pairs={{0,4},{4,8},{8,12},{12,16},{16,20},{20,24},{24,28},{1,5},{5,9},{9,... | collective-permute-start | bytes 12296 | tf_op jit(solution)/shard_map/ppermute | solution.py:24
  176.9 5.9 %collective-permute-start.10 = (f32[2,6,1,128]{3,2,1,0:T(1,128)S(1)}, f32[2,6,1,128]{3,2,1,0:T(1,128)S(1)}, u32[]{:S(2)}, u32[]{:S(2)}) collective-permute-start(f32[2,6,1,128]{3,2,1,0:T(1,128)S(1)} %get-tuple-element.13), channel_id=1, source_target_pairs={{1,0},{2,1},{3,2},{5,4},{6,5},{7,6},{9,8},{10,9},{11,10},{13,12},{... | collective-permute-start | bytes 18440 | tf_op jit(solution)/shard_map/ppermute | solution.py:26
  178.9 6.4 %collective-permute-start.11 = (f32[2,6,1,128]{3,2,1,0:T(1,128)S(1)}, f32[2,6,1,128]{3,2,1,0:T(1,128)S(1)}, u32[]{:S(2)}, u32[]{:S(2)}) collective-permute-start(f32[2,6,1,128]{3,2,1,0:T(1,128)S(1)} %get-tuple-element.14), channel_id=1, source_target_pairs={{0,1},{1,2},{2,3},{4,5},{5,6},{6,7},{8,9},{9,10},{10,11},{12,13},{... | collective-permute-start | bytes 18440 | tf_op jit(solution)/shard_map/ppermute | solution.py:24
  185.4 4.3 %collective-permute-start.12 = (f32[2,1,4,128]{3,2,1,0:T(4,128)S(1)}, f32[2,1,4,128]{3,2,1,0:T(4,128)S(1)}, u32[]{:S(2)}, u32[]{:S(2)}) collective-permute-start(f32[2,1,4,128]{3,2,1,0:T(4,128)S(1)} %get-tuple-element.20), channel_id=1, source_target_pairs={{4,0},{8,4},{12,8},{16,12},{20,16},{24,20},{28,24},{5,1},{9,5},{13... | collective-permute-start | bytes 12296 | tf_op jit(solution)/shard_map/ppermute | solution.py:26
  187.3 4.9 %collective-permute-start.13 = (f32[2,1,4,128]{3,2,1,0:T(4,128)S(1)}, f32[2,1,4,128]{3,2,1,0:T(4,128)S(1)}, u32[]{:S(2)}, u32[]{:S(2)}) collective-permute-start(f32[2,1,4,128]{3,2,1,0:T(4,128)S(1)} %get-tuple-element.19), channel_id=1, source_target_pairs={{0,4},{4,8},{8,12},{12,16},{16,20},{20,24},{24,28},{1,5},{5,9},{9,... | collective-permute-start | bytes 12296 | tf_op jit(solution)/shard_map/ppermute | solution.py:24
  192.3 5.9 %collective-permute-start.14 = (f32[2,6,1,128]{3,2,1,0:T(1,128)S(1)}, f32[2,6,1,128]{3,2,1,0:T(1,128)S(1)}, u32[]{:S(2)}, u32[]{:S(2)}) collective-permute-start(f32[2,6,1,128]{3,2,1,0:T(1,128)S(1)} %get-tuple-element.11), channel_id=1, source_target_pairs={{1,0},{2,1},{3,2},{5,4},{6,5},{7,6},{9,8},{10,9},{11,10},{13,12},{... | collective-permute-start | bytes 18440 | tf_op jit(solution)/shard_map/ppermute | solution.py:26
  194.2 6.4 %collective-permute-start.15 = (f32[2,6,1,128]{3,2,1,0:T(1,128)S(1)}, f32[2,6,1,128]{3,2,1,0:T(1,128)S(1)}, u32[]{:S(2)}, u32[]{:S(2)}) collective-permute-start(f32[2,6,1,128]{3,2,1,0:T(1,128)S(1)} %get-tuple-element.12), channel_id=1, source_target_pairs={{0,1},{1,2},{2,3},{4,5},{5,6},{6,7},{8,9},{9,10},{10,11},{12,13},{... | collective-permute-start | bytes 18440 | tf_op jit(solution)/shard_map/ppermute | solution.py:24
Sparse Core Ops, SparseCore 0:
  33.8 53.6 reduce-scatter.3
where the time goes:
time: 209 us; the launch traced here: 208 us
  waiting for transfers between devices  55.6 us (27%)
  starting transfers between devices  51.9 us (25%)
  other arithmetic  38.9 us (19%)
  local copies, waits for them, and re-layouts  26.9 us (13%)
  blocking collectives  14.4 us (7%)
  between operations  13.8 us (7%)
  matrix products  6.52 us (3%)
    unnamed x2, waiting for transfers between devices  28.3 us
    scatter-add x1, other arithmetic, per_device(): jnp.zeros((NVEC, points + 1), jnp.float32).at[:, received_places[0]]  26 us
    ppermute x8, starting transfers between devices, extended(): lax.ppermute(tail, axis, [(i, (i + 1) % count) for i in range(ends)])  23.1 us
    ppermute x8, waiting for transfers between devices, extended(): lax.ppermute(tail, axis, [(i, (i + 1) % count) for i in range(ends)])  22.2 us
    ppermute x8, starting transfers between devices, extended(): lax.ppermute(head, axis, [((i + 1) % count, i) for i in range(ends)])  18.2 us
    all_gather x1, blocking collectives, per_device(): gathered = lax.all_gather(vectors, 'row', axis=2, tiled=True)  14.4 us
    unnamed x20, local copies, waits for them, and re-layouts  14.2 us
    another operation x2, other arithmetic  9.25 us
  transfers between devices with their start and end apart: 19, of which 10 were waited for; matrix products, arithmetic and copies ran while one was open for 14% of the time, Pallas kernels for 0%

commit v1 on v0

--- a/solution.py
+++ b/solution.py
@@ -11,6 +11,13 @@
 TILE_COLS = 8
 KMAX = 8
 LEAF = 512
+
+
+def stacked_exchange(x, name, split, join):
+    size = lax.axis_size(name)
+    blocks = jnp.stack(jnp.split(x, size, axis=split), axis=0)
+    blocks = lax.all_to_all(blocks, name, split_axis=0, concat_axis=0)
+    return jnp.concatenate(blocks, axis=join)
 
 
 def extended(cells, sides, width):
@@ -90,7 +97,7 @@
     targets = lax.dynamic_slice_in_dim(cluster_perm[0], lax.axis_index("col") * points, points)
     send_values, send_places = route(summed, targets, 1, points, capacity, devices)
     received_values, received_places = (
-        lax.all_to_all(send_values, ("row", "col"), split_axis=1, concat_axis=1, tiled=True),
+        stacked_exchange(send_values, ("row", "col"), 1, 1),
         lax.all_to_all(send_places, ("row", "col"), split_axis=1, concat_axis=1, tiled=True),
     )
     field = (

time: 209 us -> 231 us (1.11)
  local copies, waits for them, and re-layouts: 26.9 us -> 48.4 us
  waiting for transfers between devices: 55.6 us -> 49.2 us
  starting transfers between devices: 51.9 us -> 56.3 us
    unnamed x20 -> x49, local copies, waits for them, and re-layouts: 14.2 us -> 33.5 us
    ppermute x8, waiting for transfers between devices: 22.2 us -> 10.5 us  [extended(): lax.ppermute(tail, axis, [(i, (i + 1) % count) for i in range(ends)])]
    ppermute x8, starting transfers between devices: 18.2 us -> 28.2 us  [extended(): lax.ppermute(head, axis, [((i + 1) % count, i) for i in range(ends)])]
    ppermute x8, starting transfers between devices: 23.1 us -> 17.4 us  [extended(): lax.ppermute(tail, axis, [(i, (i + 1) % count) for i in range(ends)])]
    ppermute x8, waiting for transfers between devices: 0.02 us -> 5.25 us  [extended(): lax.ppermute(head, axis, [((i + 1) % count, i) for i in range(ends)])]
    another operation x5 -> x7, local copies, waits for them, and re-layouts: 0.31 us -> 3.75 us  [the longest x2 3.43 us: stacked_exchange(): blocks = jnp.stack(jnp.split(x, size, axis=split), axis=0)]
    all_to_all x2 -> x0, local copies, waits for them, and re-layouts: 3.21 us -> none  [per_device(): lax.all_to_all(send_values, ('row', 'col'), split_axis=1, concat_axis=1,...]
  transfers between devices with their start and end apart: 19 -> 19, of which waited for: 10 -> 10; matrix products, arithmetic and copies ran while one was open for 14% -> 22% of each run, Pallas kernels for 0% -> 0%
where the time goes in v1:
time: 231 us; the launch traced here: 228 us
  starting transfers between devices  56.3 us (24%)
  waiting for transfers between devices  49.2 us (21%)
  local copies, waits for them, and re-layouts  48.4 us (21%)
  other arithmetic  39.6 us (17%)
  blocking collectives  14.4 us (6%)
  between operations  13.9 us (6%)
  matrix products  6.52 us (3%)
    unnamed x49, local copies, waits for them, and re-layouts  33.5 us
    unnamed x2, waiting for transfers between devices  28.3 us
    ppermute x8, starting transfers between devices, extended(): lax.ppermute(head, axis, [((i + 1) % count, i) for i in range(ends)])  28.2 us
    scatter-add x1, other arithmetic, per_device(): jnp.zeros((NVEC, points + 1), jnp.float32).at[:, received_places[0]]  26 us
    ppermute x8, starting transfers between devices, extended(): lax.ppermute(tail, axis, [(i, (i + 1) % count) for i in range(ends)])  17.4 us
    all_gather x1, blocking collectives, per_device(): gathered = lax.all_gather(vectors, 'row', axis=2, tiled=True)  14.4 us
    ppermute x8, waiting for transfers between devices, extended(): lax.ppermute(tail, axis, [(i, (i + 1) % count) for i in range(ends)])  10.5 us
    another operation x2, other arithmetic  9.25 us
  transfers between devices with their start and end apart: 19, of which 10 were waited for; matrix products, arithmetic and copies ran while one was open for 22% of the time, Pallas kernels for 0%

profile of v1, /device:TPU:12, one launch (start us, length us, event | category | flops | bytes accessed | tf_op | source)
XLA Modules:
  0.0 228.3 jit_solution(12604995572181548420)
XLA Ops:
  8.0 14.4 %all_gather.3 = bf16[2,1,16384]{2,0,1:T(2,128)(2,1)S(1)} all-gather(bf16[2,1,2048]{2,0,1:T(2,128)(2,1)} %param.8), channel_id=1, replica_groups=mesh['row'=8,'col'=4] {'row'}, dimensions={2}, use_global_device_ids=true | all-gather | bytes 73728 | tf_op jit(solution)/shard_map/all_gather | solution.py:67
  25.0 3.5 %fusion.2 = f32[2,8,512]{2,0,1:T(2,128)S(1)} fusion(bf16[1,1,8,512,512]{4,3,2,1,0:T(8,128)(2,1)} %param.12, bf16[8,2,512]{2,1,0:T(2,128)(2,1)S(1)} %gather_fusion, pred[8]{0:T(512)(128)(4,1)S(1)} %and_bitcast_fusion), kind=kOutput, calls=%fused_computation.7 | convolution fusion | flops 8396800 | bytes 4243464 | tf_op jit(solution)/shard_map/lqp,vlp->vlq/dot_general | solution.py:85
  28.9 2.8 %fusion.7 = f32[4,2,2048,1]{2,1,3,0:T(2,128)S(1)} fusion(bf16[4,8,8,2048]{3,2,1,0:T(8,128)(2,1)S(1)} %bitcast.208, bf16[2,8,2048,1]{2,0,1,3:T(2,128)(2,1)S(1)} %bitcast.215, bf16[4,8,8,2048]{3,2,1,0:T(8,128)(2,1)S(1)} %bitcast.212, f32[4,8,8]{2,1,0:T(8,128)S(1)} %fusion.74), kind=kOutput, calls=%fused_computation.11 | convolution fusion | flops 4195328 | bytes 2229248 | tf_op jit(solution)/shard_map/abkp,abvk->vap/dot_general | solution.py:79
  31.7 2.6 %copy.130 = f32[2,8192]{0,1:T(8,128)} copy(f32[2,8192]{1,0:T(2,128)S(1)} %add.151) | data formatting | bytes 131072
  35.2 9.1 %reduce-window.6 = s32[1,32,16,128]{3,2,1,0:T(8,128)S(1)} reduce-window(s32[1,32,16,128]{3,2,1,0:T(8,128)S(1)} %bitcast.211, s32[]{:T(128)} %constant.61.clone.1), window={size=1x1x1x128 pad=0_0x0_0x0_0x127_0}, to_apply=%region_0.1 | reduce-window | flops 8323072 | bytes 524292 | tf_op jit(solution)/shard_map/reduce-window
  45.5 8.6 %scatter_custom_fusion.2 = s32[4096]{0:T(1024)} fusion(s32[2048]{0:T(1024)S(1)} %broadcast_select_fusion.2, s32[2048]{0:T(1024)S(1)} %get-tuple-element.29, s32[]{:T(128)} %constant.60.clone.1), kind=kCustom, calls=%fused_computation.171 | custom fusion | bytes 16388
  54.1 5.8 %all-to-all-start = ((s32[1,32,128]{2,0,1:T(1,128)}), s32[1,32,128]{2,0,1:T(1,128)S(1)}, u32[]{:S(2)}, u32[]{:S(2)}) async-start(s32[1,32,128]{2,0,1:T(1,128)} %bitcast.7), calls=%async_computation | async-start | bytes 32768 | tf_op jit(solution)/shard_map/all_to_all | solution.py:101
  59.9 28.3 %reduce-scatter.4.cloned.1.call-done = f32[2048,2]{1,0:T(8,128)} async-done(((f32[8192,2]{1,0:T(8,128)}), f32[2048,2]{1,0:T(8,128)}) %reduce-scatter.4.cloned.1.call-update) | async-done | bytes 16400
  91.1 6.5 %scatter_custom_fusion = f32[2,4096]{0,1:T(8,128)S(1)} fusion(s32[2048]{0:T(1024)S(1)} %bitcast.219, f32[2048,2]{1,0:T(8,128)} %copy.119, f32[]{:T(128)} %constant.59.clone.1), kind=kCustom, calls=%fused_computation.12 | custom fusion | bytes 33280 | tf_op jit(solution)/shard_map/scatter | solution.py:59
  117.5 2.8 %copy.120 = f32[32,2,128]{2,1,0:T(2,128)} copy(f32[32,2,128]{1,2,0:T(8,128)} %fusion.13) | data formatting | bytes 65536 | tf_op jit(solution)/shard_map/stack | solution.py:18
  120.3 4.9 %all-to-all-start.1 = ((f32[32,2,128]{2,1,0:T(2,128)}), f32[32,2,128]{2,1,0:T(2,128)S(1)}, u32[]{:S(2)}, u32[]{:S(2)}) async-start(f32[32,2,128]{2,1,0:T(2,128)} %copy.120), calls=%async_computation.1 | async-start | bytes 65536 | tf_op jit(solution)/shard_map/all_to_all | solution.py:19
  125.2 5.1 %all-to-all-done.1 = f32[32,2,128]{2,1,0:T(2,128)S(1)} async-done(((f32[32,2,128]{2,1,0:T(2,128)}), f32[32,2,128]{2,1,0:T(2,128)S(1)}, u32[]{:S(2)}, u32[]{:S(2)}) %all-to-all-start.1) | async-done | bytes 32800 | tf_op jit(solution)/shard_map/all_to_all | solution.py:19
  130.3 2.0 copy.121
  132.3 26.0 %scatter_custom_fusion.1 = f32[2,2049]{0,1:T(8,128)S(1)} fusion(s32[4096]{0:T(1024)S(1)} %bitcast.224, f32[4096,2]{1,0:T(8,128)} %copy.121, f32[]{:T(128)} %constant.59.clone.1), kind=kCustom, calls=%fused_computation.14 | custom fusion | flops 8192 | bytes 16904 | tf_op jit(solution)/shard_map/scatter-add | solution.py:104
  158.8 3.0 %collective-permute-start = (f32[2,1,4,128]{3,2,1,0:T(4,128)S(1)}, f32[2,1,4,128]{3,2,1,0:T(4,128)S(1)}, u32[]{:S(2)}, u32[]{:S(2)}) collective-permute-start(f32[2,1,4,128]{3,2,1,0:T(4,128)S(1)} %get-tuple-element.26), channel_id=1, source_target_pairs={{4,0},{8,4},{12,8},{16,12},{20,16},{24,20},{28,24},{5,1},{9,5},{13... | collective-permute-start | bytes 12296 | tf_op jit(solution)/shard_map/ppermute | solution.py:33
  161.8 1.9 collective-permute-start.1
  163.7 3.0 %collective-permute-done.1 = f32[2,1,4,128]{3,2,1,0:T(4,128)S(1)} collective-permute-done((f32[2,1,4,128]{3,2,1,0:T(4,128)S(1)}, f32[2,1,4,128]{3,2,1,0:T(4,128)S(1)}, u32[]{:S(2)}, u32[]{:S(2)}) %collective-permute-start.1) | collective-permute-done | bytes 4128 | tf_op jit(solution)/shard_map/ppermute | solution.py:31
  166.7 2.5 %collective-permute-start.3 = (f32[2,6,1,128]{3,2,1,0:T(1,128)S(1)}, f32[2,6,1,128]{3,2,1,0:T(1,128)S(1)}, u32[]{:S(2)}, u32[]{:S(2)}) collective-permute-start(f32[2,6,1,128]{3,2,1,0:T(1,128)S(1)} %get-tuple-element.18), channel_id=1, source_target_pairs={{0,1},{1,2},{2,3},{4,5},{5,6},{6,7},{8,9},{9,10},{10,11},{12,13},{... | collective-permute-start | bytes 18440 | tf_op jit(solution)/shard_map/ppermute | solution.py:31
  169.2 4.2 %collective-permute-start.2 = (f32[2,6,1,128]{3,2,1,0:T(1,128)S(1)}, f32[2,6,1,128]{3,2,1,0:T(1,128)S(1)}, u32[]{:S(2)}, u32[]{:S(2)}) collective-permute-start(f32[2,6,1,128]{3,2,1,0:T(1,128)S(1)} %get-tuple-element.17), channel_id=1, source_target_pairs={{1,0},{2,1},{3,2},{5,4},{6,5},{7,6},{9,8},{10,9},{11,10},{13,12},{... | collective-permute-start | bytes 18440 | tf_op jit(solution)/shard_map/ppermute | solution.py:33
  174.9 1.9 collective-permute-start.4
  176.8 2.4 %collective-permute-start.5 = (f32[2,1,4,128]{3,2,1,0:T(4,128)S(1)}, f32[2,1,4,128]{3,2,1,0:T(4,128)S(1)}, u32[]{:S(2)}, u32[]{:S(2)}) collective-permute-start(f32[2,1,4,128]{3,2,1,0:T(4,128)S(1)} %get-tuple-element.23), channel_id=1, source_target_pairs={{0,4},{4,8},{8,12},{12,16},{16,20},{20,24},{24,28},{1,5},{5,9},{9,... | collective-permute-start | bytes 12296 | tf_op jit(solution)/shard_map/ppermute | solution.py:31
  179.2 2.5 %collective-permute-done.5 = f32[2,1,4,128]{3,2,1,0:T(4,128)S(1)} collective-permute-done((f32[2,1,4,128]{3,2,1,0:T(4,128)S(1)}, f32[2,1,4,128]{3,2,1,0:T(4,128)S(1)}, u32[]{:S(2)}, u32[]{:S(2)}) %collective-permute-start.5) | collective-permute-done | bytes 4128 | tf_op jit(solution)/shard_map/ppermute | solution.py:31
  181.8 1.9 collective-permute-start.7
  183.7 5.1 %collective-permute-start.6 = (f32[2,6,1,128]{3,2,1,0:T(1,128)S(1)}, f32[2,6,1,128]{3,2,1,0:T(1,128)S(1)}, u32[]{:S(2)}, u32[]{:S(2)}) collective-permute-start(f32[2,6,1,128]{3,2,1,0:T(1,128)S(1)} %get-tuple-element.15), channel_id=1, source_target_pairs={{1,0},{2,1},{3,2},{5,4},{6,5},{7,6},{9,8},{10,9},{11,10},{13,12},{... | collective-permute-start | bytes 18440 | tf_op jit(solution)/shard_map/ppermute | solution.py:33
  192.1 2.4 %collective-permute-start.9 = (f32[2,1,4,128]{3,2,1,0:T(4,128)S(1)}, f32[2,1,4,128]{3,2,1,0:T(4,128)S(1)}, u32[]{:S(2)}, u32[]{:S(2)}) collective-permute-start(f32[2,1,4,128]{3,2,1,0:T(4,128)S(1)} %get-tuple-element.21), channel_id=1, source_target_pairs={{0,4},{4,8},{8,12},{12,16},{16,20},{20,24},{24,28},{1,5},{5,9},{9,... | collective-permute-start | bytes 12296 | tf_op jit(solution)/shard_map/ppermute | solution.py:31
  194.6 2.5 %collective-permute-done.9 = f32[2,1,4,128]{3,2,1,0:T(4,128)S(1)} collective-permute-done((f32[2,1,4,128]{3,2,1,0:T(4,128)S(1)}, f32[2,1,4,128]{3,2,1,0:T(4,128)S(1)}, u32[]{:S(2)}, u32[]{:S(2)}) %collective-permute-start.9) | collective-permute-done | bytes 4128 | tf_op jit(solution)/shard_map/ppermute | solution.py:31
  197.1 1.9 collective-permute-start.11
  199.0 5.1 %collective-permute-start.10 = (f32[2,6,1,128]{3,2,1,0:T(1,128)S(1)}, f32[2,6,1,128]{3,2,1,0:T(1,128)S(1)}, u32[]{:S(2)}, u32[]{:S(2)}) collective-permute-start(f32[2,6,1,128]{3,2,1,0:T(1,128)S(1)} %get-tuple-element.13), channel_id=1, source_target_pairs={{1,0},{2,1},{3,2},{5,4},{6,5},{7,6},{9,8},{10,9},{11,10},{13,12},{... | collective-permute-start | bytes 18440 | tf_op jit(solution)/shard_map/ppermute | solution.py:33
  207.4 2.4 %collective-permute-start.13 = (f32[2,1,4,128]{3,2,1,0:T(4,128)S(1)}, f32[2,1,4,128]{3,2,1,0:T(4,128)S(1)}, u32[]{:S(2)}, u32[]{:S(2)}) collective-permute-start(f32[2,1,4,128]{3,2,1,0:T(4,128)S(1)} %get-tuple-element.19), channel_id=1, source_target_pairs={{0,4},{4,8},{8,12},{12,16},{16,20},{20,24},{24,28},{1,5},{5,9},{9,... | collective-permute-start | bytes 12296 | tf_op jit(solution)/shard_map/ppermute | solution.py:31
  209.9 2.5 %collective-permute-done.13 = f32[2,1,4,128]{3,2,1,0:T(4,128)S(1)} collective-permute-done((f32[2,1,4,128]{3,2,1,0:T(4,128)S(1)}, f32[2,1,4,128]{3,2,1,0:T(4,128)S(1)}, u32[]{:S(2)}, u32[]{:S(2)}) %collective-permute-start.13) | collective-permute-done | bytes 4128 | tf_op jit(solution)/shard_map/ppermute | solution.py:31
  212.4 1.9 collective-permute-start.15
  214.3 5.1 %collective-permute-start.14 = (f32[2,6,1,128]{3,2,1,0:T(1,128)S(1)}, f32[2,6,1,128]{3,2,1,0:T(1,128)S(1)}, u32[]{:S(2)}, u32[]{:S(2)}) collective-permute-start(f32[2,6,1,128]{3,2,1,0:T(1,128)S(1)} %get-tuple-element.11), channel_id=1, source_target_pairs={{1,0},{2,1},{3,2},{5,4},{6,5},{7,6},{9,8},{10,9},{11,10},{13,12},{... | collective-permute-start | bytes 18440 | tf_op jit(solution)/shard_map/ppermute | solution.py:33
  (108 shorter events, 39.8 us)
Async XLA Ops:
  6.5 22.3 %copy-start = (bf16[1,1,32,8,2048]{4,3,2,1,0:T(8,128)(2,1)S(1)}, bf16[1,1,32,8,2048]{4,3,2,1,0:T(8,128)(2,1)}, u32[]{:S(2)}) copy-start(bf16[1,1,32,8,2048]{4,3,2,1,0:T(8,128)(2,1)} %param.9) | copy-start | bytes 3145732
  6.5 81.6 %reduce-scatter.4.cloned.1.call-start = ((), (), s32[]{:S(2)}) async-start(), calls=%async_computation.3 | async-start | bytes 5242880
  25.0 3.9 %copy-start.1 = (bf16[1,1,32,8,2048]{4,3,2,1,0:T(8,128)(2,1)S(1)}, bf16[1,1,32,8,2048]{4,3,2,1,0:T(8,128)(2,1)}, u32[]{:S(2)}) copy-start(bf16[1,1,32,8,2048]{4,3,2,1,0:T(8,128)(2,1)} %param.10) | copy-start | bytes 3145732
  34.3 0.8 copy-start.3
  34.3 10.9 %copy-start.5 = (s32[2]{0:T(128)S(1)}, s32[2]{0:T(128)}, u32[]{:S(2)}) copy-start(s32[2]{0:T(128)} %constant.96) | copy-start | bytes 28
  34.3 11.0 %copy-start.4 = (s32[2]{0:T(128)S(1)}, s32[2]{0:T(128)}, u32[]{:S(2)}) copy-start(s32[2]{0:T(128)} %constant.93) | copy-start | bytes 28
  54.1 66.2 %all-to-all-start = ((s32[1,32,128]{2,0,1:T(1,128)}), s32[1,32,128]{2,0,1:T(1,128)S(1)}, u32[]{:S(2)}, u32[]{:S(2)}) async-start(s32[1,32,128]{2,0,1:T(1,128)} %bitcast.7), calls=%async_computation | async-start | bytes 32768 | tf_op jit(solution)/shard_map/all_to_all | solution.py:101
  120.3 10.0 %all-to-all-start.1 = ((f32[32,2,128]{2,1,0:T(2,128)}), f32[32,2,128]{2,1,0:T(2,128)S(1)}, u32[]{:S(2)}, u32[]{:S(2)}) async-start(f32[32,2,128]{2,1,0:T(2,128)} %copy.120), calls=%async_computation.1 | async-start | bytes 65536 | tf_op jit(solution)/shard_map/all_to_all | solution.py:19
  132.3 41.1 %copy-start.2 = (f32[4,4,128]{2,1,0:T(4,128)S(1)}, f32[4,4,128]{2,1,0:T(4,128)}, u32[]{:S(2)}) copy-start(f32[4,4,128]{2,1,0:T(4,128)} %param.15) | copy-start | bytes 24580
  158.8 4.9 %collective-permute-start = (f32[2,1,4,128]{3,2,1,0:T(4,128)S(1)}, f32[2,1,4,128]{3,2,1,0:T(4,128)S(1)}, u32[]{:S(2)}, u32[]{:S(2)}) collective-permute-start(f32[2,1,4,128]{3,2,1,0:T(4,128)S(1)} %get-tuple-element.26), channel_id=1, source_target_pairs={{4,0},{8,4},{12,8},{16,12},{20,16},{24,20},{28,24},{5,1},{9,5},{13... | collective-permute-start | bytes 12296 | tf_op jit(solution)/shard_map/ppermute | solution.py:33
  161.8 4.9 %collective-permute-start.1 = (f32[2,1,4,128]{3,2,1,0:T(4,128)S(1)}, f32[2,1,4,128]{3,2,1,0:T(4,128)S(1)}, u32[]{:S(2)}, u32[]{:S(2)}) collective-permute-start(f32[2,1,4,128]{3,2,1,0:T(4,128)S(1)} %get-tuple-element.25), channel_id=1, source_target_pairs={{0,4},{4,8},{8,12},{12,16},{16,20},{20,24},{24,28},{1,5},{5,9},{9,... | collective-permute-start | bytes 12296 | tf_op jit(solution)/shard_map/ppermute | solution.py:31
  166.7 6.8 %collective-permute-start.3 = (f32[2,6,1,128]{3,2,1,0:T(1,128)S(1)}, f32[2,6,1,128]{3,2,1,0:T(1,128)S(1)}, u32[]{:S(2)}, u32[]{:S(2)}) collective-permute-start(f32[2,6,1,128]{3,2,1,0:T(1,128)S(1)} %get-tuple-element.18), channel_id=1, source_target_pairs={{0,1},{1,2},{2,3},{4,5},{5,6},{6,7},{8,9},{9,10},{10,11},{12,13},{... | collective-permute-start | bytes 18440 | tf_op jit(solution)/shard_map/ppermute | solution.py:31
  169.2 5.6 %collective-permute-start.2 = (f32[2,6,1,128]{3,2,1,0:T(1,128)S(1)}, f32[2,6,1,128]{3,2,1,0:T(1,128)S(1)}, u32[]{:S(2)}, u32[]{:S(2)}) collective-permute-start(f32[2,6,1,128]{3,2,1,0:T(1,128)S(1)} %get-tuple-element.17), channel_id=1, source_target_pairs={{1,0},{2,1},{3,2},{5,4},{6,5},{7,6},{9,8},{10,9},{11,10},{13,12},{... | collective-permute-start | bytes 18440 | tf_op jit(solution)/shard_map/ppermute | solution.py:33
  174.9 4.3 %collective-permute-start.4 = (f32[2,1,4,128]{3,2,1,0:T(4,128)S(1)}, f32[2,1,4,128]{3,2,1,0:T(4,128)S(1)}, u32[]{:S(2)}, u32[]{:S(2)}) collective-permute-start(f32[2,1,4,128]{3,2,1,0:T(4,128)S(1)} %get-tuple-element.24), channel_id=1, source_target_pairs={{4,0},{8,4},{12,8},{16,12},{20,16},{24,20},{28,24},{5,1},{9,5},{13... | collective-permute-start | bytes 12296 | tf_op jit(solution)/shard_map/ppermute | solution.py:33
  176.8 4.9 %collective-permute-start.5 = (f32[2,1,4,128]{3,2,1,0:T(4,128)S(1)}, f32[2,1,4,128]{3,2,1,0:T(4,128)S(1)}, u32[]{:S(2)}, u32[]{:S(2)}) collective-permute-start(f32[2,1,4,128]{3,2,1,0:T(4,128)S(1)} %get-tuple-element.23), channel_id=1, source_target_pairs={{0,4},{4,8},{8,12},{12,16},{16,20},{20,24},{24,28},{1,5},{5,9},{9,... | collective-permute-start | bytes 12296 | tf_op jit(solution)/shard_map/ppermute | solution.py:31
  181.8 7.0 %collective-permute-start.7 = (f32[2,6,1,128]{3,2,1,0:T(1,128)S(1)}, f32[2,6,1,128]{3,2,1,0:T(1,128)S(1)}, u32[]{:S(2)}, u32[]{:S(2)}) collective-permute-start(f32[2,6,1,128]{3,2,1,0:T(1,128)S(1)} %get-tuple-element.16), channel_id=1, source_target_pairs={{0,1},{1,2},{2,3},{4,5},{5,6},{6,7},{8,9},{9,10},{10,11},{12,13},{... | collective-permute-start | bytes 18440 | tf_op jit(solution)/shard_map/ppermute | solution.py:31
  183.7 6.4 %collective-permute-start.6 = (f32[2,6,1,128]{3,2,1,0:T(1,128)S(1)}, f32[2,6,1,128]{3,2,1,0:T(1,128)S(1)}, u32[]{:S(2)}, u32[]{:S(2)}) collective-permute-start(f32[2,6,1,128]{3,2,1,0:T(1,128)S(1)} %get-tuple-element.15), channel_id=1, source_target_pairs={{1,0},{2,1},{3,2},{5,4},{6,5},{7,6},{9,8},{10,9},{11,10},{13,12},{... | collective-permute-start | bytes 18440 | tf_op jit(solution)/shard_map/ppermute | solution.py:33
  190.2 4.3 %collective-permute-start.8 = (f32[2,1,4,128]{3,2,1,0:T(4,128)S(1)}, f32[2,1,4,128]{3,2,1,0:T(4,128)S(1)}, u32[]{:S(2)}, u32[]{:S(2)}) collective-permute-start(f32[2,1,4,128]{3,2,1,0:T(4,128)S(1)} %get-tuple-element.22), channel_id=1, source_target_pairs={{4,0},{8,4},{12,8},{16,12},{20,16},{24,20},{28,24},{5,1},{9,5},{13... | collective-permute-start | bytes 12296 | tf_op jit(solution)/shard_map/ppermute | solution.py:33
  192.1 4.9 %collective-permute-start.9 = (f32[2,1,4,128]{3,2,1,0:T(4,128)S(1)}, f32[2,1,4,128]{3,2,1,0:T(4,128)S(1)}, u32[]{:S(2)}, u32[]{:S(2)}) collective-permute-start(f32[2,1,4,128]{3,2,1,0:T(4,128)S(1)} %get-tuple-element.21), channel_id=1, source_target_pairs={{0,4},{4,8},{8,12},{12,16},{16,20},{20,24},{24,28},{1,5},{5,9},{9,... | collective-permute-start | bytes 12296 | tf_op jit(solution)/shard_map/ppermute | solution.py:31
  197.1 7.0 %collective-permute-start.11 = (f32[2,6,1,128]{3,2,1,0:T(1,128)S(1)}, f32[2,6,1,128]{3,2,1,0:T(1,128)S(1)}, u32[]{:S(2)}, u32[]{:S(2)}) collective-permute-start(f32[2,6,1,128]{3,2,1,0:T(1,128)S(1)} %get-tuple-element.14), channel_id=1, source_target_pairs={{0,1},{1,2},{2,3},{4,5},{5,6},{6,7},{8,9},{9,10},{10,11},{12,13},{... | collective-permute-start | bytes 18440 | tf_op jit(solution)/shard_map/ppermute | solution.py:31
  199.0 6.4 %collective-permute-start.10 = (f32[2,6,1,128]{3,2,1,0:T(1,128)S(1)}, f32[2,6,1,128]{3,2,1,0:T(1,128)S(1)}, u32[]{:S(2)}, u32[]{:S(2)}) collective-permute-start(f32[2,6,1,128]{3,2,1,0:T(1,128)S(1)} %get-tuple-element.13), channel_id=1, source_target_pairs={{1,0},{2,1},{3,2},{5,4},{6,5},{7,6},{9,8},{10,9},{11,10},{13,12},{... | collective-permute-start | bytes 18440 | tf_op jit(solution)/shard_map/ppermute | solution.py:33
  205.5 4.3 %collective-permute-start.12 = (f32[2,1,4,128]{3,2,1,0:T(4,128)S(1)}, f32[2,1,4,128]{3,2,1,0:T(4,128)S(1)}, u32[]{:S(2)}, u32[]{:S(2)}) collective-permute-start(f32[2,1,4,128]{3,2,1,0:T(4,128)S(1)} %get-tuple-element.20), channel_id=1, source_target_pairs={{4,0},{8,4},{12,8},{16,12},{20,16},{24,20},{28,24},{5,1},{9,5},{13... | collective-permute-start | bytes 12296 | tf_op jit(solution)/shard_map/ppermute | solution.py:33
  207.4 4.9 %collective-permute-start.13 = (f32[2,1,4,128]{3,2,1,0:T(4,128)S(1)}, f32[2,1,4,128]{3,2,1,0:T(4,128)S(1)}, u32[]{:S(2)}, u32[]{:S(2)}) collective-permute-start(f32[2,1,4,128]{3,2,1,0:T(4,128)S(1)} %get-tuple-element.19), channel_id=1, source_target_pairs={{0,4},{4,8},{8,12},{12,16},{16,20},{20,24},{24,28},{1,5},{5,9},{9,... | collective-permute-start | bytes 12296 | tf_op jit(solution)/shard_map/ppermute | solution.py:31
  212.4 7.0 %collective-permute-start.15 = (f32[2,6,1,128]{3,2,1,0:T(1,128)S(1)}, f32[2,6,1,128]{3,2,1,0:T(1,128)S(1)}, u32[]{:S(2)}, u32[]{:S(2)}) collective-permute-start(f32[2,6,1,128]{3,2,1,0:T(1,128)S(1)} %get-tuple-element.12), channel_id=1, source_target_pairs={{0,1},{1,2},{2,3},{4,5},{5,6},{6,7},{8,9},{9,10},{10,11},{12,13},{... | collective-permute-start | bytes 18440 | tf_op jit(solution)/shard_map/ppermute | solution.py:31
  214.3 6.4 %collective-permute-start.14 = (f32[2,6,1,128]{3,2,1,0:T(1,128)S(1)}, f32[2,6,1,128]{3,2,1,0:T(1,128)S(1)}, u32[]{:S(2)}, u32[]{:S(2)}) collective-permute-start(f32[2,6,1,128]{3,2,1,0:T(1,128)S(1)} %get-tuple-element.11), channel_id=1, source_target_pairs={{1,0},{2,1},{3,2},{5,4},{6,5},{7,6},{9,8},{10,9},{11,10},{13,12},{... | collective-permute-start | bytes 18440 | tf_op jit(solution)/shard_map/ppermute | solution.py:33
Sparse Core Ops, SparseCore 0:
  34.5 53.6 reduce-scatter.3
